TPU v7x, 256 devices: a whole 4x4x8 slice. The times are simulated.
256 devices in a mesh: row: 32 (over y, z_hi, core), col: 8 (over z_lo, x).
Axes of the slice: x: 4, y: 4, z: 8 (z_hi: 4, z_lo: 2; z = z_hi * 2 + z_lo), core: 2. Of those that a mesh axis runs over, the one named last changes fastest.
Arguments:
- alignment: bfloat16 [64, 1024, 64], P(None, ('col', 'row')), may hold values from -6 to 6
- pair_rep: bfloat16 [1024, 1024, 128], P('row', 'col'), may hold values from -128 to 128
- outer_left: bfloat16 [64, 32], replicated, may hold values from -0.75 to 0.75
- outer_right: bfloat16 [64, 32], replicated, may hold values from -0.75 to 0.75
- outer_proj: bfloat16 [1024, 128], replicated, may hold values from -1.5 to 1.5
- outer_bias: float32 [128], replicated, may hold values from -3 to 3
- average_value: bfloat16 [64, 256], replicated, may hold values from -0.75 to 0.75
- average_gate: bfloat16 [64, 256], replicated, may hold values from -0.75 to 0.75
- average_logit: bfloat16 [128, 8], replicated, may hold values from -28 to 28
- average_out: bfloat16 [256, 64], replicated, may hold values from -1 to 1
- triangle_proj: bfloat16 [128, 512], replicated, may hold values from -0.5 to 0.5
- triangle_bias: bfloat16 [128, 4], replicated, may hold values from -0.5 to 0.5
Outputs:
- pair_new: bfloat16 [1024, 1024, 128], P('row', 'col')
- alignment_update: bfloat16 [64, 1024, 64], P(None, ('row', 'col'))
- triangle_inputs: bfloat16 [1024, 1024, 512], P(('col', 'row'))
- edge_bias: bfloat16 [4, 1024, 1024], P(None, ('col', 'row'))
All inputs are finite; a program needn't handle non-finite values.
Results may differ from a plain program's by a relative error of at most 0.02.
The roundings to bfloat16 on the way count: a program that leaves them out, or rounds other values in their place, can miss the bound.
Values may be sent and summed in bfloat16 or wider, within the bound.
No kernel may reach another device: no remote copies, remote signals or barrier semaphores. Data moves between devices by JAX's collectives and lax.ppermute only.
A program may use at most 64 MiB of HBM per device.

v0:
```python
import jax
import jax.numpy as jnp
from jax import lax
from jax.sharding import PartitionSpec as P


def broadcast(shard, axis, root):
    mine = lax.axis_index(axis) == root
    return lax.psum(jnp.where(mine, shard, jnp.zeros_like(shard)), axis)


def standardize(values):
    widened = values.astype(jnp.float32)
    centered = widened - jnp.mean(widened, axis=-1, keepdims=True)
    spread = jnp.mean(centered * centered, axis=-1, keepdims=True)
    return centered * lax.rsqrt(spread + 1e-05)


def per_device(
    alignment,
    pair_rep,
    outer_left,
    outer_right,
    outer_proj,
    outer_bias,
    average_value,
    average_gate,
    average_logit,
    average_out,
    triangle_proj,
    triangle_bias,
):
    row_devices = lax.axis_size("row")
    col_devices = lax.axis_size("col")
    local_row_index = lax.axis_index("row")
    col_index = lax.axis_index("col")
    sequence_count, slab_length, alignment_channel_width = alignment.shape
    row_window, cols_tile, pair_width = pair_rep.shape
    factor_width = outer_left.shape[1]
    head_count = average_logit.shape[1]
    value_width = average_value.shape[1]
    head_width = value_width // head_count
    alignment_layer_norm = standardize(alignment).astype(jnp.bfloat16)
    normalized_flat_rows = alignment_layer_norm.reshape(
        sequence_count, slab_length * alignment_channel_width
    )
    right_own = jnp.dot(
        alignment_layer_norm, outer_right, preferred_element_type=jnp.float32
    ).astype(jnp.bfloat16)
    value_own = jnp.dot(
        alignment_layer_norm, average_value, preferred_element_type=jnp.float32
    ).astype(jnp.bfloat16)
    normalized_columns, right_cols, value_cols = (
        lax.all_gather(normalized_flat_rows, "row", axis=1, tiled=True),
        lax.all_gather(
            right_own.reshape(sequence_count, slab_length * factor_width), "row", axis=1, tiled=True
        ),
        lax.all_gather(
            value_own.reshape(sequence_count, slab_length * value_width), "row", axis=1, tiled=True
        ),
    )
    right_cols = right_cols.reshape(sequence_count, cols_tile, factor_width)
    value_cols = value_cols.reshape(sequence_count, cols_tile, value_width)
    group_member_count = row_devices // col_devices
    start_position = local_row_index % group_member_count * (row_window * alignment_channel_width)
    local_rows = lax.dynamic_slice_in_dim(
        normalized_columns, start_position, row_window * alignment_channel_width, 1
    )
    norm_rows = broadcast(local_rows, "col", local_row_index // group_member_count).reshape(
        sequence_count, row_window, alignment_channel_width
    )
    left_rows = jnp.dot(norm_rows, outer_left, preferred_element_type=jnp.float32).astype(
        jnp.bfloat16
    )
    row_block = 8
    block_count = row_window // row_block
    left_blocks = jnp.transpose(
        left_rows.reshape(sequence_count, block_count, row_block * factor_width), (1, 0, 2)
    )
    right_flat = right_cols.reshape(sequence_count, cols_tile * factor_width)

    def pair_block(block_items):
        left_flat, pair_rows = block_items
        outer_sum = lax.dot_general(
            left_flat, right_flat, (((0,), (0,)), ((), ())), preferred_element_type=jnp.float32
        )
        outer_sum = jnp.transpose(
            outer_sum.reshape(row_block, factor_width, cols_tile, factor_width), (0, 2, 1, 3)
        )
        outer_mean = (
            outer_sum.reshape(row_block, cols_tile, factor_width * factor_width) / sequence_count
        ).astype(jnp.bfloat16)
        update = jnp.dot(outer_mean, outer_proj, preferred_element_type=jnp.float32)
        return (pair_rows.astype(jnp.float32) + update + outer_bias).astype(jnp.bfloat16)

    pair_new = lax.map(
        pair_block, (left_blocks, pair_rep.reshape(block_count, row_block, cols_tile, pair_width))
    )
    pair_new = pair_new.reshape(row_window, cols_tile, pair_width)
    pair_norm = standardize(pair_new).astype(jnp.bfloat16)
    logits = jnp.einsum("ijc,ch->hij", pair_norm, average_logit, preferred_element_type=jnp.float32)
    peak_values = lax.pmax(jnp.max(logits, axis=2), "col")
    weights = jnp.exp(logits - peak_values[:, :, None]).astype(jnp.bfloat16)
    denom_part = jnp.sum(weights.astype(jnp.float32), axis=2)
    value_heads = value_cols.reshape(sequence_count, cols_tile, head_count, head_width)
    numer_part = jnp.einsum(
        "hij,sjhc->ishc", weights, value_heads, preferred_element_type=jnp.float32
    )
    numer_part = numer_part.reshape(row_window, sequence_count, value_width)
    out_wide = average_out.astype(jnp.float32)
    numer_sub, denom_sub = (
        lax.psum_scatter(
            numer_part.astype(jnp.bfloat16), "col", scatter_dimension=0, tiled=True
        ).astype(jnp.float32),
        lax.psum_scatter(
            denom_part.astype(jnp.bfloat16), "col", scatter_dimension=1, tiled=True
        ).astype(jnp.float32),
    )
    sub_len = numer_sub.shape[0]
    norm_sub = lax.dynamic_slice_in_dim(norm_rows, col_index * sub_len, sub_len, 1)
    gate_vals = jax.nn.sigmoid(jnp.dot(norm_sub, average_gate, preferred_element_type=jnp.float32))
    gate_vals = gate_vals.reshape(sequence_count, sub_len, head_count, head_width)
    numer_moved = jnp.transpose(
        numer_sub.reshape(sub_len, sequence_count, head_count, head_width), (1, 0, 2, 3)
    )
    gated_vals = (gate_vals * numer_moved / jnp.transpose(denom_sub)[None, :, :, None]).reshape(
        sequence_count, sub_len, value_width
    )
    alignment_update = jnp.dot(gated_vals, out_wide, precision=lax.Precision.HIGHEST).astype(
        jnp.bfloat16
    )
    piece_len = cols_tile // row_devices
    shaped = pair_norm.reshape(row_window, row_devices, piece_len, pair_width)
    split_at = 3 * (triangle_proj.shape[1] // 4)
    turned = lax.all_to_all(shaped, "row", split_axis=1, concat_axis=0, tiled=True)[:, 0]
    projected = jnp.einsum("jic,cd->ijd", turned, triangle_proj, preferred_element_type=jnp.float32)
    inputs = jnp.concatenate(
        [projected[..., :split_at], jax.nn.sigmoid(projected[..., split_at:])], axis=-1
    ).astype(jnp.bfloat16)
    bias_rows = jnp.einsum(
        "jic,ch->ihj", turned, triangle_bias, preferred_element_type=jnp.float32
    ).astype(jnp.bfloat16)
    triangle_inputs, bias_rows = (inputs, bias_rows)
    edge_bias = jnp.transpose(bias_rows, (1, 0, 2))
    return (pair_new, alignment_update, triangle_inputs, edge_bias)


def solution(mesh):
    placed = (
        P(None, ("col", "row"), None),
        P("row", "col", None),
        P(),
        P(),
        P(),
        P(),
        P(),
        P(),
        P(),
        P(),
        P(),
        P(),
    )
    return jax.shard_map(
        per_device,
        mesh=mesh,
        in_specs=placed,
        out_specs=(
            P("row", "col", None),
            P(None, ("row", "col"), None),
            P(("col", "row"), None, None),
            P(None, ("col", "row"), None),
        ),
        check_vma=False,
    )
```

profile of v0, /device:TPU:16, one launch (start us, length us, event | category | flops | bytes accessed | tf_op | source)
XLA Modules:
  0.0 337.7 jit_solution(5402792686740338694)
XLA Ops:
  7.2 1.0 convert_reduce_fusion.1
  8.2 1.1 fusion.22
  9.3 1.0 fusion.23
  10.4 0.7 reshape.113
  11.2 53.5 %all-gather.3.cloned.1.call-done = bf16[64,8192]{1,0:T(8,128)(2,1)} async-done(((bf16[64,256]{1,0:T(8,128)(2,1)}), bf16[64,8192]{1,0:T(8,128)(2,1)}) %all-gather.3.cloned.1.call-update) | async-done | bytes 1048592 | tf_op jit(solution)/shard_map/all_gather | solution.py:54
  64.7 1.0 dynamic-slice_select_fusion
  65.7 0.5 reshape.114
  66.3 1.0 copy.76
  67.4 0.2 fusion.14
  67.5 0.6 copy.102
  68.2 0.2 convolution_convert_fusion.3
  68.4 41.0 %all_gather.10 = bf16[64,4096]{0,1:T(8,128)(2,1)S(1)} all-gather(bf16[64,128]{0,1:T(8,128)(2,1)S(1)} %bitcast.144), channel_id=1, replica_groups=mesh['row'=32,'col'=8] {'row'}, dimensions={1}, use_global_device_ids=true | all-gather | bytes 540672 | tf_op jit(solution)/shard_map/all_gather | solution.py:55
  109.4 37.8 %all-reduce.3.cloned.1.call-done = bf16[64,32,64]{2,0,1:T(8,128)(2,1)} async-done(((bf16[64,32,64]{2,0,1:T(8,128)(2,1)}), bf16[64,32,64]{2,0,1:T(8,128)(2,1)}) %all-reduce.3.cloned.1.call-update) | async-done | bytes 262160 | tf_op jit(solution)/shard_map/psum | solution.py:9
  147.1 1.6 convolution_convert_fusion
  148.8 17.9 %while.10 = (s32[]{:T(128)}, bf16[4,8,128,128]{3,2,1,0:T(8,128)(2,1)S(1)}, bf16[4,8,128,128]{3,2,1,0:T(8,128)(2,1)}, bf16[4,64,256]{1,2,0:T(8,128)(2,1)S(1)}, bf...) while((s32[]{:T(128)}, ...), condition=%wide.region_4.5_spmd, body=%wide.region_3.4_spmd.sunk | while | flops 405274624 | bytes 10846821 | solution.py:96
  148.8 1.1 copy.111
  149.9 0.7 fusion.59
  150.6 0.8 copy.112
  151.4 1.8 fusion.60
  153.3 1.1 copy.111
  154.4 0.7 fusion.59
  155.1 0.8 copy.112
  155.9 1.8 fusion.60
  157.8 1.1 copy.111
  158.9 0.7 fusion.59
  159.6 0.8 copy.112
  160.4 1.8 fusion.60
  162.2 1.1 copy.111
  163.4 0.7 fusion.59
  164.1 0.8 copy.112
  164.9 1.8 fusion.60
  166.7 1.9 copy.86
  168.6 0.3 convert_reduce_fusion
  169.0 0.1 copy.87
  169.2 1.3 multiply_reduce_fusion
  170.6 0.2 rsqrt.26
  170.8 0.2 div.52
  171.0 3.3 multiply_convert_fusion.1
  174.3 9.3 %all-to-all-start = ((bf16[32,32,4,128]{3,0,2,1:T(8,128)(2,1)}), bf16[32,32,4,128]{3,0,2,1:T(8,128)(2,1)S(1)}, u32[]{:S(2)}, u32[]{:S(2)}) async-start(bf16[32,32,4,128]{3,0,2,1:T(8,128)(2,1)} %multiply_convert_fusion.1), calls=%async_computation.1 | async-start | bytes 2097152 | tf_op jit(solution)/shard_map/all_to_all | solution.py:135
  183.6 2.1 fusion.41
  185.7 55.5 %pmax.7 = f32[8,32]{0,1:T(8,128)S(1)} all-reduce(f32[8,32]{0,1:T(8,128)S(1)} %get-tuple-element.76), channel_id=1, replica_groups=mesh['row'=32,'col'=8] {'col'}, use_global_device_ids=true, to_apply=%region_8.9 | all-reduce | flops 256 | bytes 2048 | tf_op jit(solution)/shard_map/pmax | solution.py:102
  241.4 8.4 %copy.81 = bf16[64,32768]{0,1:T(8,128)(2,1)} copy(bf16[64,32768]{1,0:T(8,128)(2,1)} %all-gather.5.cloned.1.call-done) | data formatting | bytes 8388608 | tf_op jit(solution)/shard_map/all_gather | solution.py:58
  249.8 14.8 %copy.82 = bf16[64,128,8,32]{1,3,0,2:T(8,128)(2,1)} copy(bf16[64,128,8,32]{0,3,2,1:T(8,128)(2,1)} %bitcast.130) | data formatting | bytes 8388608 | tf_op jit(solution)/shard_map/reshape;reshape | solution.py:105
  264.6 5.4 %convert_bitcast_fusion = bf16[32,64,8,32]{0,3,1,2:T(8,128)(2,1)} fusion(bf16[64,128,8,32]{1,3,0,2:T(8,128)(2,1)} %copy.82, bf16[8,32,128,1]{2,0,1,3:T(8,128)(2,1)S(1)} %fusion.33), kind=kOutput, calls=%fused_computation.12 | convolution fusion | flops 134742016 | bytes 5308416 | tf_op jit(solution)/shard_map/hij,sjhc->ishc/dot_general | solution.py:106
  269.9 8.1 %copy.84 = bf16[32,64,8,32]{1,3,2,0:T(8,128)(2,1)} copy(bf16[32,64,8,32]{0,3,1,2:T(8,128)(2,1)} %convert_bitcast_fusion) | data formatting | bytes 2097152 | tf_op jit(solution)/shard_map/convert_element_type | solution.py:113
  278.1 0.6 copy-done.12
  278.7 0.6 dynamic-slice
  280.0 1.0 fusion.13
  281.0 0.2 copy.78
  281.2 0.2 fusion.32
  281.4 18.6 %all-reduce = bf16[8,32]{0,1:T(8,128)(2,1)S(1)} all-reduce(bf16[8,32]{0,1:T(8,128)(2,1)S(1)} %fusion.32), channel_id=3, replica_groups=mesh['row'=32,'col'=8] {'col'}, use_global_device_ids=true, to_apply=%region_11.12.clone | all-reduce | flops 256 | bytes 1024
  300.1 1.0 copy-done.2
  301.1 1.3 copy.89
  302.4 1.3 convolution_bitcast_fusion
  303.7 0.5 slice.21
  304.2 0.6 fusion.10
  304.8 2.4 pad_maximum_fusion
  307.1 6.2 %copy.92 = bf16[4,1024,512]{2,1,0:T(8,128)(2,1)} copy(bf16[4,1024,512]{1,2,0:T(8,128)(2,1)} %pad_maximum_fusion) | data formatting | bytes 8388608
  313.4 0.4 fusion.15
  313.7 0.6 copy.93
  314.4 14.4 %reduce-scatter.2.cloned.1.call-done = bf16[4,64,256]{1,2,0:T(8,128)(2,1)} async-done(((bf16[32,64,256]{1,2,0:T(8,128)(2,1)}), bf16[4,64,256]{1,2,0:T(8,128)(2,1)}) %reduce-scatter.2.cloned.1.call-update) | async-done | bytes 131088 | tf_op jit(solution)/shard_map/reduce_scatter | solution.py:112
  328.8 1.1 fusion.19
  329.9 0.6 convolution_convert_fusion.2
  330.5 0.7 copy.91
  (46 shorter events, 0.7 us)
Async XLA Ops:
  7.2 295.2 %copy-start = (bf16[128,512]{1,0:T(8,128)(2,1)S(1)}, bf16[128,512]{1,0:T(8,128)(2,1)}, u32[]{:S(2)}) copy-start(bf16[128,512]{1,0:T(8,128)(2,1)} %param.24) | copy-start | bytes 393220
  7.2 60.2 %copy-start.3 = (bf16[64,256]{1,0:T(8,128)(2,1)S(1)}, bf16[64,256]{1,0:T(8,128)(2,1)}, u32[]{:S(2)}) copy-start(bf16[64,256]{1,0:T(8,128)(2,1)} %param.20) | copy-start | bytes 98308
  7.2 57.5 %all-gather.3.cloned.1.call-start = ((), (), s32[]{:S(2)}) async-start(), calls=%async_computation.2 | async-start | bytes 1081344 | tf_op jit(solution)/shard_map/all_gather | solution.py:54
  8.2 60.0 %copy-start.6 = (bf16[64,32]{0,1:T(8,128)(2,1)S(1)}, bf16[64,32]{0,1:T(8,128)(2,1)}, u32[]{:S(2)}) copy-start(bf16[64,32]{0,1:T(8,128)(2,1)} %param.17) | copy-start | bytes 12292
  11.1 136.0 %all-reduce.3.cloned.1.call-start = ((), (), s32[]{:S(2)}) async-start(), calls=%async_computation.3 | async-start | bytes 1048576 | tf_op jit(solution)/shard_map/psum | solution.py:9
  65.7 81.4 %copy-start.5 = (bf16[64,32]{0,1:T(8,128)(2,1)S(1)}, bf16[64,32]{0,1:T(8,128)(2,1)}, u32[]{:S(2)}) copy-start(bf16[64,32]{0,1:T(8,128)(2,1)} %param.16) | copy-start | bytes 12292
  66.3 82.5 %copy-start.8 = (bf16[1024,128]{1,0:T(8,128)(2,1)S(1)}, bf16[1024,128]{1,0:T(8,128)(2,1)}, u32[]{:S(2)}) copy-start(bf16[1024,128]{1,0:T(8,128)(2,1)} %param.18) | copy-start | bytes 786436
  66.3 82.5 %copy-start.11 = (f32[128]{0:T(128)S(1)}, f32[128]{0:T(128)}, u32[]{:S(2)}) copy-start(f32[128]{0:T(128)} %param.19) | copy-start | bytes 1540
  67.3 174.1 %all-gather.5.cloned.1.call-start = ((), (), s32[]{:S(2)}) async-start(), calls=%async_computation.4 | async-start | bytes 4325376 | tf_op jit(solution)/shard_map/all_gather | solution.py:58
  166.7 16.9 %copy-start.1 = (bf16[4,8,128,128]{3,2,1,0:T(8,128)(2,1)}, bf16[4,8,128,128]{3,2,1,0:T(8,128)(2,1)S(1)}, u32[]{:S(2)}) copy-start(bf16[4,8,128,128]{3,2,1,0:T(8,128)(2,1)S(1)} %get-tuple-element.41) | copy-start | bytes 3145732
  171.0 12.6 %copy-start.10 = (bf16[128,8]{0,1:T(8,128)(2,1)S(1)}, bf16[128,8]{0,1:T(8,128)(2,1)}, u32[]{:S(2)}) copy-start(bf16[128,8]{0,1:T(8,128)(2,1)} %param.22) | copy-start | bytes 6148
  174.3 125.8 %all-to-all-start = ((bf16[32,32,4,128]{3,0,2,1:T(8,128)(2,1)}), bf16[32,32,4,128]{3,0,2,1:T(8,128)(2,1)S(1)}, u32[]{:S(2)}, u32[]{:S(2)}) async-start(bf16[32,32,4,128]{3,0,2,1:T(8,128)(2,1)} %multiply_convert_fusion.1), calls=%async_computation.1 | async-start | bytes 2097152 | tf_op jit(solution)/shard_map/all_to_all | solution.py:135
  183.5 145.3 %reduce-scatter.2.cloned.1.call-start = ((), (), s32[]{:S(2)}) async-start(), calls=%async_computation.5 | async-start | bytes 2359296 | tf_op jit(solution)/shard_map/reduce_scatter | solution.py:112
  278.0 0.7 copy-start.12
  278.1 1.9 copy-start.9
  300.1 1.0 copy-start.2
  307.1 6.2 %copy-start.7 = (bf16[128,4]{0,1:T(4,128)(2,1)S(1)}, bf16[128,4]{0,1:T(4,128)(2,1)}, u32[]{:S(2)}) copy-start(bf16[128,4]{0,1:T(4,128)(2,1)} %param.25) | copy-start | bytes 3076
  313.4 16.5 %copy-start.4 = (bf16[256,64]{0,1:T(8,128)(2,1)S(1)}, bf16[256,64]{0,1:T(8,128)(2,1)}, u32[]{:S(2)}) copy-start(bf16[256,64]{0,1:T(8,128)(2,1)} %param.23) | copy-start | bytes 98308
Sparse Core Ops, SparseCore 0:
  11.3 53.4 all-gather.2
  67.9 79.1 all-reduce.2
  149.8 74.9 all-gather.4
  278.2 50.5 reduce-scatter.1
where the time goes:
time: 339 us; the launch traced here: 338 us
  blocking collectives  115 us (34%)
  waiting for transfers between devices  106 us (31%)
  local copies, waits for them, and re-layouts  56.4 us (17%)
  matrix products  22.7 us (7%)
  between operations  14.8 us (4%)
  other arithmetic  13.3 us (4%)
  starting transfers between devices  9.42 us (3%)
    pmax x1, blocking collectives, per_device(): peak_values = lax.pmax(jnp.max(logits, axis=2), 'col')  55.5 us
    all_gather x1, waiting for transfers between devices, per_device(): lax.all_gather(normalized_flat_rows, 'row', axis=1, tiled=True)  53.5 us
    all_gather x1, blocking collectives, per_device(): lax.all_gather(right_own.reshape(sequence_count, slab_length * factor_wid...  41 us
    psum x1, waiting for transfers between devices, broadcast(): return lax.psum(jnp.where(mine, shard, jnp.zeros_like(shard)), axis)  37.8 us
    unnamed x1, blocking collectives  18.6 us
    another operation x1, local copies, waits for them, and re-layouts, per_device(): value_cols.reshape(sequence_count, cols_tile, head_count, head_width)  14.8 us
    reduce_scatter x1, waiting for transfers between devices, per_device(): lax.psum_scatter(numer_part.astype(jnp.bfloat16), 'col', scatter_dimensio...  14.4 us
    unnamed x30, local copies, waits for them, and re-layouts  9.84 us
  transfers between devices with their start and end apart: 5, of which 3 were waited for; matrix products, arithmetic and copies ran while one was open for 24% of the time, Pallas kernels for 0%

commit v1 on v0

--- a/solution.py
+++ b/solution.py
@@ -2,6 +2,13 @@
 import jax.numpy as jnp
 from jax import lax
 from jax.sharding import PartitionSpec as P
+
+
+def gather_over(x, mesh_axis, dim):
+    n_dev = lax.axis_size(mesh_axis)
+    blocks = jnp.stack([x for _ in range(n_dev)])
+    blocks = lax.all_to_all(blocks, mesh_axis, split_axis=0, concat_axis=0)
+    return jnp.concatenate(blocks, axis=dim)
 
 
 def broadcast(shard, axis, root):
@@ -51,7 +58,7 @@
         alignment_layer_norm, average_value, preferred_element_type=jnp.float32
     ).astype(jnp.bfloat16)
     normalized_columns, right_cols, value_cols = (
-        lax.all_gather(normalized_flat_rows, "row", axis=1, tiled=True),
+        gather_over(normalized_flat_rows, "row", 1),
         lax.all_gather(
             right_own.reshape(sequence_count, slab_length * factor_width), "row", axis=1, tiled=True
         ),

time: 339 us -> 317 us (0.935)
  waiting for transfers between devices: 106 us -> 81.1 us
  starting transfers between devices: 9.42 us -> 22 us
  blocking collectives: 115 us -> 103 us
    all_gather x1 -> x0, waiting for transfers between devices: 53.5 us -> none  [per_device(): lax.all_gather(normalized_flat_rows, 'row', axis=1, tiled=True)]
    all_to_all x0 -> x1, waiting for transfers between devices: none -> 27.2 us  [gather_over(): blocks = lax.all_to_all(blocks, mesh_axis, split_axis=0, concat_axis=0)]
    all_to_all x0 -> x1, starting transfers between devices: none -> 11.6 us  [gather_over(): blocks = lax.all_to_all(blocks, mesh_axis, split_axis=0, concat_axis=0)]
    pmax x1, blocking collectives: 55.5 us -> 46.3 us  [per_device(): peak_values = lax.pmax(jnp.max(logits, axis=2), 'col')]
    psum x1, waiting for transfers between devices: 37.8 us -> 41.2 us  [broadcast(): return lax.psum(jnp.where(mine, shard, jnp.zeros_like(shard)), axis)]
  transfers between devices with their start and end apart: 5 -> 5, of which waited for: 3 -> 3; matrix products, arithmetic and copies ran while one was open for 24% -> 26% of each run, Pallas kernels for 0% -> 0%
where the time goes in v1:
time: 317 us; the launch traced here: 315 us
  blocking collectives  103 us (32%)
  waiting for transfers between devices  81.1 us (26%)
  local copies, waits for them, and re-layouts  56.9 us (18%)
  matrix products  22.7 us (7%)
  starting transfers between devices  22 us (7%)
  between operations  16.6 us (5%)
  other arithmetic  12.4 us (4%)
    pmax x1, blocking collectives, per_device(): peak_values = lax.pmax(jnp.max(logits, axis=2), 'col')  46.3 us
    psum x1, waiting for transfers between devices, broadcast(): return lax.psum(jnp.where(mine, shard, jnp.zeros_like(shard)), axis)  41.2 us
    all_gather x1, blocking collectives, per_device(): lax.all_gather(right_own.reshape(sequence_count, slab_length * factor_wid...  40.3 us
    all_to_all x1, waiting for transfers between devices, gather_over(): blocks = lax.all_to_all(blocks, mesh_axis, split_axis=0, concat_axis=0)  27.2 us
    unnamed x1, blocking collectives  16.7 us
    another operation x1, local copies, waits for them, and re-layouts, per_device(): value_cols.reshape(sequence_count, cols_tile, head_count, head_width)  14.8 us
    reduce_scatter x1, waiting for transfers between devices, per_device(): lax.psum_scatter(numer_part.astype(jnp.bfloat16), 'col', scatter_dimensio...  12.7 us
    all_to_all x1, starting transfers between devices, gather_over(): blocks = lax.all_to_all(blocks, mesh_axis, split_axis=0, concat_axis=0)  11.6 us
  transfers between devices with their start and end apart: 5, of which 3 were waited for; matrix products, arithmetic and copies ran while one was open for 26% of the time, Pallas kernels for 0%

profile of v1, /device:TPU:16, one launch (start us, length us, event | category | flops | bytes accessed | tf_op | source)
XLA Modules:
  0.0 315.2 jit_solution(9470477640377772255)
XLA Ops:
  8.0 1.0 convert_reduce_fusion.1
  9.0 1.1 fusion.22
  10.1 1.0 fusion.23
  11.3 1.1 stack.3
  12.4 11.6 %all-to-all-start = ((bf16[32,64,256]{2,1,0:T(8,128)(2,1)}), bf16[32,64,256]{2,1,0:T(8,128)(2,1)S(1)}, u32[]{:S(2)}, u32[]{:S(2)}) async-start(bf16[32,64,256]{2,1,0:T(8,128)(2,1)} %stack.3), calls=%async_computation | async-start | bytes 2097152 | tf_op jit(solution)/shard_map/all_to_all | solution.py:10
  24.1 27.2 %all-to-all-done = bf16[32,64,256]{2,1,0:T(8,128)(2,1)S(1)} async-done(((bf16[32,64,256]{2,1,0:T(8,128)(2,1)}), bf16[32,64,256]{2,1,0:T(8,128)(2,1)S(1)}, u32[]{:S(2)}, u32[]{:S(2)}) %all-to-all-start) | async-done | bytes 1048608 | tf_op jit(solution)/shard_map/all_to_all | solution.py:10
  51.4 0.5 reshape.120
  52.0 1.0 copy.98
  53.0 0.2 fusion.14
  53.2 0.7 copy.125
  53.9 0.2 convolution_convert_fusion.3
  54.1 40.3 %all_gather.6 = bf16[64,4096]{0,1:T(8,128)(2,1)S(1)} all-gather(bf16[64,128]{0,1:T(8,128)(2,1)S(1)} %bitcast.149), channel_id=1, replica_groups=mesh['row'=32,'col'=8] {'row'}, dimensions={1}, use_global_device_ids=true | all-gather | bytes 540672 | tf_op jit(solution)/shard_map/all_gather | solution.py:62
  94.4 41.2 %all-reduce.3.cloned.1.call-done = bf16[64,32,64]{2,0,1:T(8,128)(2,1)} async-done(((bf16[64,32,64]{2,0,1:T(8,128)(2,1)}), bf16[64,32,64]{2,0,1:T(8,128)(2,1)}) %all-reduce.3.cloned.1.call-update) | async-done | bytes 262160 | tf_op jit(solution)/shard_map/psum | solution.py:16
  135.6 1.6 convolution_convert_fusion
  137.3 17.9 %while.10 = (s32[]{:T(128)}, bf16[4,8,128,128]{3,2,1,0:T(8,128)(2,1)S(1)}, bf16[4,8,128,128]{3,2,1,0:T(8,128)(2,1)}, bf16[4,64,256]{1,2,0:T(8,128)(2,1)S(1)}, bf...) while((s32[]{:T(128)}, ...), condition=%wide.region_4.5_spmd, body=%wide.region_3.4_spmd.sunk | while | flops 405274624 | bytes 10846821 | solution.py:103
  137.3 1.1 copy.134
  138.4 0.7 fusion.59
  139.1 0.8 copy.135
  139.9 1.8 fusion.60
  141.8 1.1 copy.134
  142.9 0.7 fusion.59
  143.6 0.8 copy.135
  144.4 1.8 fusion.60
  146.2 1.1 copy.134
  147.4 0.7 fusion.59
  148.0 0.8 copy.135
  148.9 1.8 fusion.60
  150.7 1.1 copy.134
  151.8 0.7 fusion.59
  152.5 0.8 copy.135
  153.3 1.8 fusion.60
  155.2 1.9 copy.108
  157.1 0.3 convert_reduce_fusion
  157.5 0.1 copy.109
  157.6 1.3 multiply_reduce_fusion
  159.1 0.2 rsqrt.26
  159.3 0.2 div.52
  159.5 3.3 %multiply_convert_fusion.1 = bf16[32,32,4,128]{3,0,2,1:T(8,128)(2,1)} fusion(f32[32,32,4,128]{3,0,2,1:T(8,128)} %bitcast.139, f32[32,32,4]{0,2,1:T(4,128)S(1)} %rsqrt.26, f32[32,32,4]{0,2,1:T(4,128)S(1)} %div.52), kind=kLoop, calls=%fused_computation.18 | loop fusion | flops 1572864 | bytes 3178496 | tf_op jit(solution)/shard_map/convert_element_type | solution.py:107
  162.7 10.2 %all-to-all-start.1 = ((bf16[32,32,4,128]{3,0,2,1:T(8,128)(2,1)}), bf16[32,32,4,128]{3,0,2,1:T(8,128)(2,1)S(1)}, u32[]{:S(2)}, u32[]{:S(2)}) async-start(bf16[32,32,4,128]{3,0,2,1:T(8,128)(2,1)} %multiply_convert_fusion.1), calls=%async_computation.2 | async-start | bytes 2097152 | tf_op jit(solution)/shard_map/all_to_all | solution.py:142
  173.1 2.1 fusion.41
  175.2 46.3 %pmax.7 = f32[8,32]{0,1:T(8,128)S(1)} all-reduce(f32[8,32]{0,1:T(8,128)S(1)} %get-tuple-element.80), channel_id=1, replica_groups=mesh['row'=32,'col'=8] {'col'}, use_global_device_ids=true, to_apply=%region_8.9 | all-reduce | flops 256 | bytes 2048 | tf_op jit(solution)/shard_map/pmax | solution.py:109
  221.6 8.4 %copy.103 = bf16[64,32768]{0,1:T(8,128)(2,1)} copy(bf16[64,32768]{1,0:T(8,128)(2,1)} %all-gather.2.cloned.1.call-done) | data formatting | bytes 8388608 | tf_op jit(solution)/shard_map/all_gather | solution.py:65
  230.0 14.8 %copy.104 = bf16[64,128,8,32]{1,3,0,2:T(8,128)(2,1)} copy(bf16[64,128,8,32]{0,3,2,1:T(8,128)(2,1)} %bitcast.133) | data formatting | bytes 8388608 | tf_op jit(solution)/shard_map/reshape;reshape | solution.py:112
  244.8 5.4 %convert_bitcast_fusion = bf16[32,64,8,32]{0,3,1,2:T(8,128)(2,1)} fusion(bf16[64,128,8,32]{1,3,0,2:T(8,128)(2,1)} %copy.104, bf16[8,32,128,1]{2,0,1,3:T(8,128)(2,1)S(1)} %fusion.33), kind=kOutput, calls=%fused_computation.12 | convolution fusion | flops 134742016 | bytes 5308416 | tf_op jit(solution)/shard_map/hij,sjhc->ishc/dot_general | solution.py:113
  250.2 8.1 %copy.106 = bf16[32,64,8,32]{1,3,2,0:T(8,128)(2,1)} copy(bf16[32,64,8,32]{0,3,1,2:T(8,128)(2,1)} %convert_bitcast_fusion) | data formatting | bytes 2097152 | tf_op jit(solution)/shard_map/convert_element_type | solution.py:120
  258.3 0.6 copy-done.12
  259.0 0.6 dynamic-slice
  260.2 1.0 fusion.13
  261.3 0.2 copy.100
  261.5 0.2 fusion.32
  261.7 16.7 %all-reduce = bf16[8,32]{0,1:T(8,128)(2,1)S(1)} all-reduce(bf16[8,32]{0,1:T(8,128)(2,1)S(1)} %fusion.32), channel_id=3, replica_groups=mesh['row'=32,'col'=8] {'col'}, use_global_device_ids=true, to_apply=%region_11.12.clone | all-reduce | flops 256 | bytes 1024
  278.4 1.0 copy-done.2
  279.4 1.3 copy.111
  280.7 1.3 convolution_bitcast_fusion
  282.0 0.5 slice.21
  282.5 0.6 fusion.10
  283.1 2.4 pad_maximum_fusion
  285.5 6.2 %copy.114 = bf16[4,1024,512]{2,1,0:T(8,128)(2,1)} copy(bf16[4,1024,512]{1,2,0:T(8,128)(2,1)} %pad_maximum_fusion) | data formatting | bytes 8388608
  291.7 0.4 fusion.15
  292.1 0.6 copy.115
  292.7 12.7 %reduce-scatter.2.cloned.1.call-done = bf16[4,64,256]{1,2,0:T(8,128)(2,1)} async-done(((bf16[32,64,256]{1,2,0:T(8,128)(2,1)}), bf16[4,64,256]{1,2,0:T(8,128)(2,1)}) %reduce-scatter.2.cloned.1.call-update) | async-done | bytes 131088 | tf_op jit(solution)/shard_map/reduce_scatter | solution.py:119
  305.4 1.1 fusion.19
  306.5 0.6 convolution_convert_fusion.2
  307.1 0.7 copy.113
  (47 shorter events, 0.9 us)
Async XLA Ops:
  8.0 272.7 %copy-start = (bf16[128,512]{1,0:T(8,128)(2,1)S(1)}, bf16[128,512]{1,0:T(8,128)(2,1)}, u32[]{:S(2)}) copy-start(bf16[128,512]{1,0:T(8,128)(2,1)} %param.24) | copy-start | bytes 393220
  12.4 38.9 %all-to-all-start = ((bf16[32,64,256]{2,1,0:T(8,128)(2,1)}), bf16[32,64,256]{2,1,0:T(8,128)(2,1)S(1)}, u32[]{:S(2)}, u32[]{:S(2)}) async-start(bf16[32,64,256]{2,1,0:T(8,128)(2,1)} %stack.3), calls=%async_computation | async-start | bytes 2097152 | tf_op jit(solution)/shard_map/all_to_all | solution.py:10
  24.0 111.6 %all-reduce.3.cloned.1.call-start = ((), (), s32[]{:S(2)}) async-start(), calls=%async_computation.3 | async-start | bytes 1048576 | tf_op jit(solution)/shard_map/psum | solution.py:16
  51.2 1.8 copy-start.3
  51.3 2.6 copy-start.6
  51.4 84.2 %copy-start.5 = (bf16[64,32]{0,1:T(8,128)(2,1)S(1)}, bf16[64,32]{0,1:T(8,128)(2,1)}, u32[]{:S(2)}) copy-start(bf16[64,32]{0,1:T(8,128)(2,1)} %param.16) | copy-start | bytes 12292
  51.9 85.3 %copy-start.8 = (bf16[1024,128]{1,0:T(8,128)(2,1)S(1)}, bf16[1024,128]{1,0:T(8,128)(2,1)}, u32[]{:S(2)}) copy-start(bf16[1024,128]{1,0:T(8,128)(2,1)} %param.18) | copy-start | bytes 786436
  51.9 85.3 %copy-start.11 = (f32[128]{0:T(128)S(1)}, f32[128]{0:T(128)}, u32[]{:S(2)}) copy-start(f32[128]{0:T(128)} %param.19) | copy-start | bytes 1540
  53.0 168.7 %all-gather.2.cloned.1.call-start = ((), (), s32[]{:S(2)}) async-start(), calls=%async_computation.4 | async-start | bytes 4325376 | tf_op jit(solution)/shard_map/all_gather | solution.py:65
  155.2 17.9 %copy-start.1 = (bf16[4,8,128,128]{3,2,1,0:T(8,128)(2,1)}, bf16[4,8,128,128]{3,2,1,0:T(8,128)(2,1)S(1)}, u32[]{:S(2)}) copy-start(bf16[4,8,128,128]{3,2,1,0:T(8,128)(2,1)S(1)} %get-tuple-element.41) | copy-start | bytes 3145732
  159.4 13.6 %copy-start.10 = (bf16[128,8]{0,1:T(8,128)(2,1)S(1)}, bf16[128,8]{0,1:T(8,128)(2,1)}, u32[]{:S(2)}) copy-start(bf16[128,8]{0,1:T(8,128)(2,1)} %param.22) | copy-start | bytes 6148
  162.7 115.7 %all-to-all-start.1 = ((bf16[32,32,4,128]{3,0,2,1:T(8,128)(2,1)}), bf16[32,32,4,128]{3,0,2,1:T(8,128)(2,1)S(1)}, u32[]{:S(2)}, u32[]{:S(2)}) async-start(bf16[32,32,4,128]{3,0,2,1:T(8,128)(2,1)} %multiply_convert_fusion.1), calls=%async_computation.2 | async-start | bytes 2097152 | tf_op jit(solution)/shard_map/all_to_all | solution.py:142
  173.0 132.4 %reduce-scatter.2.cloned.1.call-start = ((), (), s32[]{:S(2)}) async-start(), calls=%async_computation.5 | async-start | bytes 2359296 | tf_op jit(solution)/shard_map/reduce_scatter | solution.py:119
  258.3 0.7 copy-start.12
  258.3 1.9 copy-start.9
  278.4 1.0 copy-start.2
  285.5 6.2 %copy-start.7 = (bf16[128,4]{0,1:T(4,128)(2,1)S(1)}, bf16[128,4]{0,1:T(4,128)(2,1)}, u32[]{:S(2)}) copy-start(bf16[128,4]{0,1:T(4,128)(2,1)} %param.25) | copy-start | bytes 3076
  291.7 14.8 %copy-start.4 = (bf16[256,64]{0,1:T(8,128)(2,1)S(1)}, bf16[256,64]{0,1:T(8,128)(2,1)}, u32[]{:S(2)}) copy-start(bf16[256,64]{0,1:T(8,128)(2,1)} %param.23) | copy-start | bytes 98308
Sparse Core Ops, SparseCore 0:
  53.1 82.4 all-reduce.2
  258.4 46.9 reduce-scatter.1
Sparse Core Ops, SparseCore 1:
  56.1 59.8 all-gather.1
